TPU v7x, 128 devices: a whole 4x4x4 slice. The times are simulated.
128 devices in a mesh: row: 8 (over y, core), col: 16 (over z, x).
Axes of the slice: x: 4, y: 4, z: 4, core: 2. Of those that a mesh axis runs over, the one named last changes fastest.
Arguments:
- text_features: bfloat16 [5, 4096, 3584], P(None, ('row', 'col')), may hold values from -18 to 18
- vision_features: bfloat16 [6, 4096, 1024], P(None, ('row', 'col')), may hold values from -18 to 18
Outputs:
- stimulus_terms: float32 [4096, 30], P(('row', 'col'))
- cka: float32 [5, 6], replicated
All inputs are finite; a program needn't handle non-finite values.
Results may differ from a plain program's by a relative error of at most 0.0003.
Values may be sent and summed in bfloat16 or wider, within the bound.
A program may use at most 192 MiB of HBM per device.

v0:
```python
import functools

import jax
import jax.numpy as jnp
from jax import lax
from jax.sharding import Mesh
from jax.sharding import PartitionSpec as P

ROW = ("row_0", "row_1")
COL = ("col_0", "col_1")
ROW_COL = ("row_0", "row_1", "col_0", "col_1")


def from_everyone(shard, axis):
    copies = jnp.broadcast_to(shard, (lax.axis_size(axis), *shard.shape))
    return lax.all_to_all(copies, axis, split_axis=0, concat_axis=0, tiled=True)


def of_everyone(shard, axis):
    everything = from_everyone(shard, axis)
    return jnp.sum(everything, axis=0)


def packed_total(arrays, axis):
    ends = [0]
    for a in arrays:
        ends.append(ends[-1] + a.size)
    running = of_everyone(jnp.concatenate([a.ravel() for a in arrays]), axis)
    return tuple((running[b:e].reshape(a.shape) for a, b, e in zip(arrays, ends, ends[1:])))


def by_axis(shard, axes):
    return functools.reduce(lax.psum, axes, shard)


def cut_along(shard, dim, devices):
    before, after = (shard.shape[:dim], shard.shape[dim + 1 :])
    return jnp.moveaxis(shard.reshape(*before, devices, -1, *after), dim, 0)


def summed_on_arrival(shard, axis, dim):
    devices = lax.axis_size(axis)
    parts = lax.all_to_all(cut_along(shard, dim, devices), axis, 0, 0, tiled=True)
    return jnp.sum(parts, axis=0)


def center_with(features, totals, stimuli_count):
    values = features.astype(jnp.float32)
    return (values - totals[:, None, :] / stimuli_count).astype(jnp.bfloat16)


def local(text_features, vision_features):
    text_layers = text_features.shape[0]
    vision_layers = vision_features.shape[0]
    stimuli_count = text_features.shape[1] * lax.axis_size(ROW) * lax.axis_size(COL)
    text_block, vision_block = (
        lax.all_gather(text_features, COL, axis=1, tiled=True),
        lax.all_gather(vision_features, COL, axis=1, tiled=True),
    )
    text_set, vision_set = (
        lax.all_gather(text_features, ROW, axis=1, tiled=True),
        lax.all_gather(vision_features, ROW, axis=1, tiled=True),
    )
    text_total, vision_total = packed_total(
        (
            jnp.sum(text_block.astype(jnp.float32), axis=1),
            jnp.sum(vision_block.astype(jnp.float32), axis=1),
        ),
        ROW,
    )
    text_block = center_with(text_block, text_total, stimuli_count)
    text_set = center_with(text_set, text_total, stimuli_count)
    vision_block = center_with(vision_block, vision_total, stimuli_count)
    vision_set = center_with(vision_set, vision_total, stimuli_count)
    text_tiles = jnp.einsum(
        "lrd,lcd->lrc", text_block, text_set, preferred_element_type=jnp.float32
    )
    vision_tiles = jnp.einsum(
        "lrd,lcd->lrc", vision_block, vision_set, preferred_element_type=jnp.float32
    )
    row_share = jnp.einsum(
        "arc,brc->rab", text_tiles, vision_tiles, precision=lax.Precision.HIGHEST
    )
    block_rows = row_share.shape[0]
    cross_part = jnp.sum(row_share, axis=0)
    text_part = jnp.sum(text_tiles * text_tiles, axis=(1, 2))
    vision_part = jnp.sum(vision_tiles * vision_tiles, axis=(1, 2))
    cross, text_self, vision_self = (
        by_axis(cross_part, ROW_COL),
        by_axis(text_part, ROW_COL),
        by_axis(vision_part, ROW_COL),
    )
    own_share = summed_on_arrival(
        row_share.reshape(block_rows, text_layers * vision_layers), COL, 0
    )
    scale = 1.0 / jnp.sqrt(text_self[:, None] * vision_self[None, :])
    stimulus_terms = own_share * (scale.reshape(1, text_layers * vision_layers) * stimuli_count)
    return (stimulus_terms, cross * scale)


def solution(mesh):
    split = Mesh(mesh.devices.reshape(4, 2, 4, 4), ("row_0", "row_1", "col_0", "col_1"))
    placed = (P(None, ROW_COL, None), P(None, ROW_COL, None))
    return jax.shard_map(
        local, mesh=split, in_specs=placed, out_specs=(P(ROW_COL, None), P()), check_vma=False
    )
```

profile of v0, /device:TPU:1, one launch (start us, length us, event | category | flops | bytes accessed | tf_op | source)
XLA Modules:
  0.0 358.1 jit_solution(3340388469952081525)
XLA Ops:
  7.2 0.7 all-gather.7.cloned.1.call-update
  7.9 0.7 all-gather.5.cloned.1.call-update
  8.7 0.7 all-gather.11.cloned.1.call-update
  9.4 0.0 all-gather.9.cloned.1.call-start
  9.4 0.5 all-gather.9.cloned.1.call-update
  10.0 64.6 %all-gather.7.cloned.1.call-done = bf16[6,512,1024]{2,1,0:T(8,128)(2,1)} async-done(((bf16[6,32,1024]{2,1,0:T(8,128)(2,1)}), bf16[6,512,1024]{2,1,0:T(8,128)(2,1)}) %all-gather.7.cloned.1.call-update) | async-done | bytes 6291472 | tf_op jit(solution)/shard_map/all_gather | solution.py:58
  74.6 4.2 %convert_reduce_fusion.1 = f32[6,1024]{1,0:T(8,128)S(1)} fusion(bf16[6,512,1024]{2,1,0:T(8,128)(2,1)} %all-gather.7.cloned.1.call-done), kind=kLoop, calls=%fused_computation.7 | loop fusion | flops 6285312 | bytes 6316032 | tf_op jit(solution)/shard_map/reduce_sum | solution.py:67
  78.8 116.9 %all-gather.5.cloned.1.call-done = bf16[5,512,3584]{2,1,0:T(8,128)(2,1)} async-done(((bf16[5,32,3584]{2,1,0:T(8,128)(2,1)}), bf16[5,512,3584]{2,1,0:T(8,128)(2,1)}) %all-gather.5.cloned.1.call-update) | async-done | bytes 18350096 | tf_op jit(solution)/shard_map/all_gather | solution.py:57
  195.7 7.2 %convert_reduce_fusion = f32[5,3584]{1,0:T(8,128)S(1)} fusion(bf16[5,512,3584]{2,1,0:T(8,128)(2,1)} %all-gather.5.cloned.1.call-done), kind=kLoop, calls=%fused_computation.1 | loop fusion | flops 18332160 | bytes 18421760 | tf_op jit(solution)/shard_map/reduce_sum | solution.py:66
  203.0 0.4 broadcast_in_dim.2
  203.4 25.5 %all_to_all.11 = f32[8,1,24064]{2,1,0:T(1,128)S(1)} all-to-all(f32[8,1,24064]{2,1,0:T(1,128)S(1)} %broadcast_in_dim.2), channel_id=1, replica_groups=mesh['row_0'=4,'row_1'=2,'col_0'=4,'col_1'=4] {'row_0','row_1'}, dimensions={0} | all-to-all | bytes 1540096 | tf_op jit(solution)/shard_map/all_to_all | solution.py:16
  228.9 0.6 reduce_sum.65
  229.5 4.1 %all-gather.11.cloned.1.call-done = bf16[6,256,1024]{2,1,0:T(8,128)(2,1)} async-done(((bf16[6,32,1024]{2,1,0:T(8,128)(2,1)}), bf16[6,256,1024]{2,1,0:T(8,128)(2,1)}) %all-gather.11.cloned.1.call-update) | async-done | bytes 3145744 | tf_op jit(solution)/shard_map/all_gather | solution.py:62
  233.6 7.3 %multiply_reduce_fusion = (f32[6]{0:T(128)S(1)}, f32[6,512,256]{2,1,0:T(8,128)}) fusion(bf16[6,256,1024]{2,1,0:T(8,128)(2,1)} %all-gather.11.cloned.1.call-done, f32[6,1024]{1,0:T(8,128)S(1)} %div.16, bf16[6,512,1024]{2,1,0:T(8,128)(2,1)} %all-gather.7.cloned.1.call-done), kind=kOutput, calls=%fused_computation.16 | convolution fusion | flops 1626341376 | bytes 12607512 | tf_op jit(solution)/shard_map/lrd,lcd->lrc/dot_general | solution.py:78
  240.8 46.6 %all-gather.9.cloned.1.call-done = bf16[5,256,3584]{2,1,0:T(8,128)(2,1)} async-done(((bf16[5,32,3584]{2,1,0:T(8,128)(2,1)}), bf16[5,256,3584]{2,1,0:T(8,128)(2,1)}) %all-gather.9.cloned.1.call-update) | async-done | bytes 9175056 | tf_op jit(solution)/shard_map/all_gather | solution.py:61
  287.4 14.1 %multiply_reduce_fusion.1 = (f32[5]{0:T(128)S(1)}, f32[5,512,256]{2,1,0:T(8,128)}) fusion(bf16[5,256,3584]{2,1,0:T(8,128)(2,1)} %all-gather.9.cloned.1.call-done, f32[5,3584]{1,0:T(8,128)S(1)} %div.14, bf16[5,512,3584]{2,1,0:T(8,128)(2,1)} %all-gather.5.cloned.1.call-done), kind=kOutput, calls=%fused_computation.18 | convolution fusion | flops 4740218880 | bytes 30218260 | tf_op jit(solution)/shard_map/lrd,lcd->lrc/dot_general | solution.py:75
  301.5 10.1 %fusion.15 = (f32[5,6]{1,0:T(8,128)S(1)}, f32[512,5,6]{2,1,0:T(8,128)S(1)}) fusion(f32[6,512,256]{2,1,0:T(8,128)} %get-tuple-element.23, f32[5,512,256]{2,1,0:T(8,128)} %get-tuple-element.25), kind=kOutput, calls=%fused_computation.26 | convolution fusion | flops 47201248 | bytes 5828728 | tf_op jit(solution)/shard_map/arc,brc->rab/dot_general | solution.py:81
  311.6 0.4 reshape.56
  312.0 0.2 copy.25
  312.2 0.8 reshape.57
  313.0 6.7 %all-to-all-start.1 = ((f32[16,1,960]{2,1,0:T(1,128)}), f32[16,1,960]{2,1,0:T(1,128)S(1)}, u32[]{:S(2)}, u32[]{:S(2)}) async-start(f32[16,1,960]{2,1,0:T(1,128)} %reshape.57), calls=%async_computation.1 | async-start | bytes 131072 | tf_op jit(solution)/shard_map/all_to_all | solution.py:43
  319.6 7.4 %all-reduce.2 = (f32[6]{0:T(128)S(1)}, f32[5]{0:T(128)S(1)}, f32[5,6]{1,0:T(8,128)S(1)}) all-reduce(f32[6]{0:T(128)S(1)} %get-tuple-element.22, f32[5]{0:T(128)S(1)} %get-tuple-element.24, f32[5,6]{1,0:T(8,128)S(1)} %get-tuple-element.26), channel_id=1, replica_groups=mesh['row_0'=4,'row_1'=2,'col_0'=4,'col_1'=4] {'row_0'}, use_global_device_ids=true, to_apply=%region_10.0 | all-reduce | flops 41 | bytes 328 | tf_op jit(solution)/shard_map/psum | solution.py:33
  327.0 4.1 %all-reduce.3 = (f32[6]{0:T(128)S(1)}, f32[5]{0:T(128)S(1)}, f32[5,6]{1,0:T(8,128)S(1)}) all-reduce(f32[6]{0:T(128)S(1)} %get-tuple-element.14, f32[5]{0:T(128)S(1)} %get-tuple-element.15, f32[5,6]{1,0:T(8,128)S(1)} %get-tuple-element.16), channel_id=1, replica_groups=mesh['row_0'=4,'row_1'=2,'col_0'=4,'col_1'=4] {'row_1'}, use_global_device_ids=true, to_apply=%region_11.0 | all-reduce | flops 41 | bytes 328 | tf_op jit(solution)/shard_map/psum | solution.py:33
  331.2 8.9 %all-reduce.1 = (f32[6]{0:T(128)S(1)}, f32[5]{0:T(128)S(1)}, f32[5,6]{1,0:T(8,128)S(1)}) all-reduce(f32[6]{0:T(128)S(1)} %get-tuple-element.17, f32[5]{0:T(128)S(1)} %get-tuple-element.18, f32[5,6]{1,0:T(8,128)S(1)} %get-tuple-element.19), channel_id=1, replica_groups=mesh['row_0'=4,'row_1'=2,'col_0'=4,'col_1'=4] {'col_0'}, use_global_device_ids=true, to_apply=%region_12.0 | all-reduce | flops 41 | bytes 328 | tf_op jit(solution)/shard_map/psum | solution.py:33
  340.1 8.5 %all-reduce = (f32[6]{0:T(128)S(1)}, f32[5]{0:T(128)S(1)}, f32[5,6]{1,0:T(8,128)S(1)}) all-reduce(f32[6]{0:T(128)S(1)} %get-tuple-element.11, f32[5]{0:T(128)S(1)} %get-tuple-element.12, f32[5,6]{1,0:T(8,128)S(1)} %get-tuple-element.13), channel_id=1, replica_groups=mesh['row_0'=4,'row_1'=2,'col_0'=4,'col_1'=4] {'col_1'}, use_global_device_ids=true, to_apply=%region_13.0 | all-reduce | flops 41 | bytes 328 | tf_op jit(solution)/shard_map/psum | solution.py:33
  348.6 0.7 fusion.13
  349.2 0.1 mul.53
  349.3 0.5 broadcast.46
  349.8 0.8 reduce.1
  350.6 0.1 reshape.58
  350.8 0.1 broadcast_multiply_fusion
  350.9 0.7 copy.27
  (12 shorter events, 0.2 us)
Async XLA Ops:
  7.2 67.4 %all-gather.7.cloned.1.call-start = ((), (), s32[]{:S(2)}) async-start(), calls=%async_computation.3 | async-start | bytes 6684672 | tf_op jit(solution)/shard_map/all_gather | solution.py:58
  7.9 187.8 %all-gather.5.cloned.1.call-start = ((), (), s32[]{:S(2)}) async-start(), calls=%async_computation.2 | async-start | bytes 19496960 | tf_op jit(solution)/shard_map/all_gather | solution.py:57
  8.6 224.9 %all-gather.11.cloned.1.call-start = ((), (), s32[]{:S(2)}) async-start(), calls=%async_computation.5 | async-start | bytes 3538944 | tf_op jit(solution)/shard_map/all_gather | solution.py:62
  9.4 278.0 %all-gather.9.cloned.1.call-start = ((), (), s32[]{:S(2)}) async-start(), calls=%async_computation.4 | async-start | bytes 10321920 | tf_op jit(solution)/shard_map/all_gather | solution.py:61
  313.0 36.4 %all-to-all-start.1 = ((f32[16,1,960]{2,1,0:T(1,128)}), f32[16,1,960]{2,1,0:T(1,128)S(1)}, u32[]{:S(2)}, u32[]{:S(2)}) async-start(f32[16,1,960]{2,1,0:T(1,128)} %reshape.57), calls=%async_computation.1 | async-start | bytes 131072 | tf_op jit(solution)/shard_map/all_to_all | solution.py:43
Sparse Core Ops, SparseCore 0:
  10.1 64.4 all-gather.6
  76.7 118.9 all-gather.4
  197.4 36.0 all-gather.10
  235.1 52.2 all-gather.8
where the time goes:
time: 361 us; the launch traced here: 358 us
  waiting for transfers between devices  235 us (65%)
  blocking collectives  54.4 us (15%)
  matrix products  31.5 us (9%)
  between operations  13.9 us (4%)
  other arithmetic  13.5 us (4%)
  starting transfers between devices  6.81 us (2%)
    all_gather x1, waiting for transfers between devices, local(): lax.all_gather(text_features, COL, axis=1, tiled=True)  117 us
    all_gather x1, waiting for transfers between devices, local(): lax.all_gather(vision_features, COL, axis=1, tiled=True)  64.6 us
    all_gather x1, waiting for transfers between devices, local(): lax.all_gather(text_features, ROW, axis=1, tiled=True)  46.6 us
    psum x4, blocking collectives, by_axis(): return functools.reduce(lax.psum, axes, shard)  28.9 us
    all_to_all x1, blocking collectives, from_everyone(): return lax.all_to_all(copies, axis, split_axis=0, concat_axis=0, tiled=True)  25.5 us
    dot_general x1, matrix products, local(): jnp.einsum('lrd,lcd->lrc', text_block, text_set, preferred_element_type=j...  14.1 us
    dot_general x1, matrix products, local(): jnp.einsum('arc,brc->rab', text_tiles, vision_tiles, precision=lax.Precis...  10.1 us
    dot_general x1, matrix products, local(): jnp.einsum('lrd,lcd->lrc', vision_block, vision_set, preferred_element_ty...  7.26 us
  transfers between devices with their start and end apart: 5, of which 4 were waited for; matrix products, arithmetic and copies ran while one was open for 6% of the time, Pallas kernels for 0%

commit v1 on v0

v1 whole, which is shorter than its diff:
```python
import jax
import jax.numpy as jnp
from jax import lax
from jax.experimental import pallas as pl
from jax.experimental.pallas import tpu as pltpu
from jax.sharding import Mesh
from jax.sharding import PartitionSpec as P

STIMULI = 4096
LA, LB = 5, 6
BLOCKS = (
    (0, 1, 0), (0, 0, 2), (3, 0, 0), (2, 0, 0), (1, 3, 0), (1, 1, 1),
    (0, 1, 1), (0, 1, 2), (0, 0, 0), (2, 3, 0), (0, 0, 3), (0, 3, 0),
)
OWN = 8
STRIPS = ((2, 4, 5, 10, 11), (1, 5, 10, 11), (0, 1, 3, 7, 8, 10, 11), (1, 3, 4, 9, 11), (0, 1, 5, 6, 10), (3, 4, 5, 6, 9, 10))
STEPS = ((1, 0, 0), (3, 0, 0), (0, 1, 0), (0, 3, 0), (0, 0, 1), (0, 0, 3))
EDGES = (
    ((8, 0, 2), (8, 2, 1), (8, 10, 5), (8, 11, 3)),
    ((10, 1, 5), (2, 3, 1), (11, 4, 0), (0, 6, 4)),
    ((6, 5, 0), (1, 7, 2), (3, 9, 3)),
)
CHUNKS, WIDTH = 24, 512
ROWS, HALF = 64, 32
ALL = len(BLOCKS) * ROWS
AHEAD, LAG, LATE = 3, 2, 2
LAST = (3, 10, 17, 19, 21, 23)
F32, BF16 = jnp.float32, jnp.bfloat16
MESH = pl.DeviceIdType.MESH


def kernel(
    text, vision, terms, cka,
    buf, acc, rx, xc, sums, mrx, rs, selfs, rrx, row, ar1, ar2,
    load_sem, swap_send, swap_recv, mean_send, mean_recv, hop_send, hop_recv,
    ex_send, ex_recv, rs_send, rs_recv, ar1_send, ar1_recv, ar2_send, ar2_recv,
):
    y, p = lax.axis_index("row_0"), lax.axis_index("row_1")
    z, x = lax.axis_index("col_0"), lax.axis_index("col_1")

    def at(offset, core):
        dx, dy, dz = offset
        return (lax.rem(y + dy, 4), core, lax.rem(z + dz, 4), lax.rem(x + dx, 4))

    def back(step):
        return tuple((4 - v) % 4 for v in step)

    def remote(src, dst, send, recv, device):
        return pltpu.make_async_remote_copy(
            src_ref=src, dst_ref=dst, send_sem=send, recv_sem=recv, device_id=device, device_id_type=MESH
        )

    other = 1 - p
    here = (0, 0, 0)

    def source(c, core):
        if c < 4:
            return text.at[2, :, pl.ds(pl.multiple_of(core * 1536 + c * WIDTH, WIDTH), WIDTH)]
        if c < 11:
            return text.at[core * 3, :, pl.ds((c - 4) * WIDTH, WIDTH)]
        if c < 18:
            return text.at[core * 3 + 1, :, pl.ds((c - 11) * WIDTH, WIDTH)]
        return vision.at[core * 3 + (c - 18) // 2, :, pl.ds((c - 18) % 2 * WIDTH, WIDTH)]

    mine = pl.ds(pl.multiple_of(OWN * ROWS + p * HALF, HALF), HALF)

    def load(c):
        return pltpu.make_async_copy(source(c, p), buf.at[c, mine, :], load_sem.at[c])

    def swap(c):
        return remote(source(c, other), buf.at[c, mine, :], swap_send.at[c], swap_recv.at[c], at(here, other))

    for c in range(CHUNKS):
        if c == 0:
            pl.when(p == 0)(lambda: load(0).start())
            pl.when(p == 1)(lambda: swap(0).start())
        else:
            load(c).start()
            swap(c).start()

    @pl.loop(0, 36)
    def _(i):
        acc[i // 6, i % 6] = jnp.zeros((ALL, 128), F32)

    rs[...] = jnp.zeros_like(rs)
    selfs[...] = jnp.zeros_like(selfs)

    sums[0, 0:1, :] = jnp.zeros((1, WIDTH), F32)
    ones = jnp.ones((8, ROWS), BF16)

    @pl.loop(p, CHUNKS)
    def _(c):
        part = buf.at[c, mine, :]
        pltpu.make_async_copy(part, part, load_sem.at[c]).wait()
        pltpu.make_async_copy(part, part, swap_recv.at[c]).wait()
        total = jnp.dot(ones, buf[c, OWN * ROWS : (OWN + 1) * ROWS, :], preferred_element_type=F32)
        sums[0, pl.ds(c, 1), :] = total[0:1]

    def hop(edge, c):
        held, becomes, step = edge
        return remote(
            buf.at[c, pl.ds(held * ROWS, ROWS), :],
            buf.at[c, pl.ds(becomes * ROWS, ROWS), :],
            hop_send.at[c],
            hop_recv.at[c, becomes],
            at(back(STEPS[step]), p),
        )

    def arrived(block, c):
        part = buf.at[c, pl.ds(block * ROWS, ROWS), :]
        pltpu.make_async_copy(part, part, hop_recv.at[c, block]).wait()

    def send_own(c):
        for edge in EDGES[0]:
            hop(edge, c).start()

    def mean_copy(axis, k):
        offset = tuple(k if i == axis else 0 for i in range(3))
        return remote(
            sums.at[axis], mrx.at[axis, k - 1], mean_send.at[axis, k - 1], mean_recv.at[axis, k - 1], at(offset, p)
        )

    for axis in range(3):
        for k in (1, 2, 3):
            mean_copy(axis, k).start()
        if axis == 0:
            pl.when(p == 0)(lambda: send_own(0))
        else:
            send_own(axis)
        for k in (1, 2, 3):
            mean_copy(axis, k).wait_recv()
        sums[axis + 1] = (sums[axis] + mrx[axis, 0]) + (mrx[axis, 1] + mrx[axis, 2])

    inner = [sorted({e[0] for e in EDGES[d]}) for d in range(3)]
    leaves = [e[1] for d in EDGES for e in d if all(e[1] not in s for s in inner)]

    def exchange(layer):
        return remote(
            acc.at[layer, pl.ds(other * 3, 3)], rx.at[layer], ex_send.at[layer], ex_recv.at[layer], at(here, other)
        )

    def compute(c):
        for block in leaves:
            arrived(block, c)
        mean = sums[3, pl.ds(c, 1), :] * (1.0 / STIMULI)
        xc[...] = (buf[c].astype(F32) - mean).astype(BF16)
        layer = jnp.where(c < 4, 0, jnp.where(c < 11, 1, jnp.where(c < 18, 2, 3 + (c - 18) // 2)))
        for g in range(3):
            tile = lax.dot_general(
                xc[...],
                xc[g * 256 : (g + 1) * 256, :],
                (((1,), (1,)), ((), ())),
                preferred_element_type=F32,
            )
            acc[layer, 2 * g] += tile[:, :128]
            acc[layer, 2 * g + 1] += tile[:, 128:]
        for layer, last in enumerate(LAST):
            pl.when(c == last)(lambda layer=layer: exchange(layer).start())

    @pl.loop(min(AHEAD, LAG), CHUNKS + 2 * LAG + LATE)
    def _(u):
        @pl.when((u >= AHEAD) & (u < CHUNKS))
        def _():
            send_own(u)

        for depth in (1, 2):
            c = u - depth * LAG

            @pl.when((c >= p) & (c < CHUNKS))
            def _():
                for block in inner[depth]:
                    arrived(block, c)
                for edge in EDGES[depth]:
                    hop(edge, c).start()

        c = u - 2 * LAG - LATE

        @pl.when((c >= p) & (c < CHUNKS))
        def _():
            compute(c)

    for layer in range(6):
        exchange(layer).wait_recv()

    def products(core):
        texts = (0, 1, 2, 3, 4) if core == 0 else (3, 4, 2, 0, 1)
        for i in range(3):
            q = core * 3 + i
            for k in range(3):
                n_text = LA if k == 0 else 0

                def body(r, sums_):
                    s = list(sums_)
                    for block in STRIPS[q]:
                        at_ = pl.ds(pl.multiple_of(block * ROWS + r * 8, 8), 8)
                        t = (
                            acc[1, q, at_, :],
                            acc[2, q, at_, :],
                            acc[0, q, at_, :] + rx[0, i, at_, :],
                            rx[1, i, at_, :],
                            rx[2, i, at_, :],
                        )
                        v = (acc[3 + k, q, at_, :], rx[3 + k, i, at_, :])
                        for a in range(LA):
                            for b in range(2):
                                s[2 * a + b] += t[a] * v[b]
                        for b in range(2):
                            s[10 + b] += v[b] * v[b]
                        for a in range(n_text):
                            s[12 + a] += t[a] * t[a]
                    return tuple(s)

                zero = jnp.zeros((8, 128), F32)
                s = lax.fori_loop(0, 8, body, (zero,) * (12 + n_text))
                visions = (core * 3 + k, (1 - core) * 3 + k)
                for a in range(LA):
                    for b in range(2):
                        n = texts[a] * LB + visions[b]
                        rs[i, n : n + 1, :] = jnp.sum(s[2 * a + b], axis=0, keepdims=True)
                for b in range(2):
                    n = 8 + visions[b]
                    selfs[n : n + 1, :] += jnp.sum(s[10 + b], axis=0, keepdims=True)
                for a in range(n_text):
                    n = texts[a]
                    selfs[n : n + 1, :] += jnp.sum(s[12 + a], axis=0, keepdims=True)

            for j in (2 * q, 2 * q + 1):
                for to in (0, 1):
                    if j == OWN and to == core:
                        rrx[j] = rs[i]
                    else:
                        share(i, j, to).start()

    def share(i, j, to):
        return remote(rs.at[i], rrx.at[j], rs_send.at[i, j % 2, to], rs_recv.at[j], at(BLOCKS[j], to))

    for core in (0, 1):
        pl.when(p == core)(lambda core=core: products(core))

    cross = rs[0] + rs[1] + rs[2]
    parts = jnp.concatenate([cross, selfs[...]], axis=0)
    parts = jnp.sum(parts, axis=1, keepdims=True)
    lane = lax.broadcasted_iota(jnp.int32, (48, 128), 1)
    sub = lax.broadcasted_iota(jnp.int32, (48, 128), 0)
    row[0] = jnp.sum(jnp.where(lane == sub, parts, 0.0), axis=0, keepdims=True)

    plane = [(dx, dy) for dx in range(4) for dy in range(4) if dx or dy]
    me1 = x * 4 + y

    def over_plane(n):
        dx, dy = plane[n]
        return remote(row.at[0], ar1.at[me1], ar1_send.at[n], ar1_recv.at[me1], at((dx, dy, 0), p))

    for n in range(15):
        over_plane(n).start()
    ar1[me1] = row[0]
    for dx, dy in plane:
        n = lax.rem(x + dx, 4) * 4 + lax.rem(y + dy, 4)
        pltpu.make_async_copy(ar1.at[n], ar1.at[n], ar1_recv.at[n]).wait()
    row[1] = jnp.sum(ar1[...], axis=0)

    column = [(dz, dc) for dz in range(4) for dc in range(2) if dz or dc]
    me2 = z * 2 + p

    def over_column(n):
        dz, dc = column[n]
        return remote(
            row.at[1], ar2.at[me2], ar2_send.at[n], ar2_recv.at[me2], at((0, 0, dz), other if dc else p)
        )

    for n in range(7):
        over_column(n).start()
    ar2[me2] = row[1]
    for dz, dc in column:
        n = lax.rem(z + dz, 4) * 2 + (other if dc else p)
        pltpu.make_async_copy(ar2.at[n], ar2.at[n], ar2_recv.at[n]).wait()
    total = jnp.sum(ar2[...], axis=0)

    def pick(index, n):
        lanes = lax.broadcasted_iota(jnp.int32, (n, 128), 1)
        return jnp.sum(jnp.where(lanes == index, total, 0.0), axis=1, keepdims=True)

    pair = lax.broadcasted_iota(jnp.int32, (32, 1), 0)
    of_text, of_vision = pair // LB, lax.rem(pair, LB)
    scale = 1.0 / jnp.sqrt(pick(32 + jnp.minimum(of_text, LA - 1), 32) * pick(40 + of_vision, 32))
    for j in range(len(BLOCKS)):
        if j == OWN:
            pl.when(p != OWN // 6)(lambda: pltpu.make_async_copy(rrx.at[OWN], rrx.at[OWN], rs_recv.at[OWN]).wait())
        else:
            pltpu.make_async_copy(rrx.at[j], rrx.at[j], rs_recv.at[j]).wait()
    even = ((rrx[0] + rrx[2]) + (rrx[4] + rrx[6])) + (rrx[8] + rrx[10])
    odd = ((rrx[1] + rrx[3]) + (rrx[5] + rrx[7])) + (rrx[9] + rrx[11])
    share_sum = even + pltpu.roll(odd, 64, 1)
    share_sum = jnp.where(p == 0, share_sum, pltpu.roll(share_sum, 96, 1))
    out = jnp.transpose(share_sum * (scale * STIMULI))
    terms[...] = out[:HALF, : LA * LB]

    a_sub = lax.broadcasted_iota(jnp.int32, (8, 1), 0)
    spread = jnp.broadcast_to(total, (8, 128))
    crosses = spread
    for a in range(1, LA):
        crosses = jnp.where(a_sub == a, pltpu.roll(spread, 128 - a * LB, 1), crosses)
    text_self = pick(32 + jnp.minimum(a_sub, LA - 1), 8)
    vision_self = pltpu.roll(spread, 128 - 40, 1)
    ratio = crosses[:LA, :LB] * (1.0 / jnp.sqrt(text_self[:LA] * vision_self[:LA, :LB]))
    cka[...] = ratio

    for c in range(CHUNKS):
        if c == 0:
            pl.when(p == 1)(lambda: swap(0).wait_send())
        else:
            swap(c).wait_send()
    for axis in range(3):
        for k in (1, 2, 3):
            mean_copy(axis, k).wait_send()

    @pl.loop(p, CHUNKS)
    def _(c):
        part = buf.at[c, pl.ds(0, ALL - ROWS), :]
        pltpu.make_async_copy(part, part, hop_send.at[c]).wait()

    for layer in range(6):
        exchange(layer).wait_send()

    def drain(core):
        for i in range(3):
            q = core * 3 + i
            for j in (2 * q, 2 * q + 1):
                for to in (0, 1):
                    if not (j == OWN and to == core):
                        share(i, j, to).wait_send()

    for core in (0, 1):
        pl.when(p == core)(lambda core=core: drain(core))
    for n in range(15):
        over_plane(n).wait_send()
    for n in range(7):
        over_column(n).wait_send()


def local(text_features, vision_features):
    dma = pltpu.SemaphoreType.DMA
    return pl.pallas_call(
        kernel,
        out_shape=(
            jax.ShapeDtypeStruct((HALF, LA * LB), F32),
            jax.ShapeDtypeStruct((LA, LB), F32),
        ),
        in_specs=[pl.BlockSpec(memory_space=pl.ANY)] * 2,
        out_specs=(pl.BlockSpec(memory_space=pltpu.VMEM), pl.BlockSpec(memory_space=pltpu.VMEM)),
        scratch_shapes=[
            pltpu.VMEM((CHUNKS, ALL, WIDTH), BF16),
            pltpu.VMEM((6, 6, ALL, 128), F32),
            pltpu.VMEM((6, 3, ALL, 128), F32),
            pltpu.VMEM((ALL, WIDTH), BF16),
            pltpu.VMEM((4, CHUNKS, WIDTH), F32),
            pltpu.VMEM((3, 3, CHUNKS, WIDTH), F32),
            pltpu.VMEM((3, 32, 128), F32),
            pltpu.VMEM((16, 128), F32),
            pltpu.VMEM((12, 32, 128), F32),
            pltpu.VMEM((2, 1, 128), F32),
            pltpu.VMEM((16, 1, 128), F32),
            pltpu.VMEM((8, 1, 128), F32),
            dma((CHUNKS,)),
            dma((CHUNKS,)),
            dma((CHUNKS,)),
            dma((3, 3)),
            dma((3, 3)),
            dma((CHUNKS,)),
            dma((CHUNKS, len(BLOCKS))),
            dma((6,)),
            dma((6,)),
            dma((3, 2, 2)),
            dma((12,)),
            dma((15,)),
            dma((16,)),
            dma((7,)),
            dma((8,)),
        ],
        compiler_params=pltpu.CompilerParams(has_side_effects=True, vmem_limit_bytes=60 * 2**20),
    )(text_features, vision_features)


def solution(mesh):
    split = Mesh(mesh.devices.reshape(4, 2, 4, 4), ("row_0", "row_1", "col_0", "col_1"))
    rows = ("row_0", "row_1", "col_0", "col_1")
    placed = (P(None, rows, None), P(None, rows, None))
    return jax.shard_map(local, mesh=split, in_specs=placed, out_specs=(P(rows, None), P()), check_vma=False)
```

time: 361 us -> 123 us (0.34)
  waiting for transfers between devices: 235 us -> 0 us
  Pallas kernels: 0 us -> 120 us
  blocking collectives: 54.4 us -> 0 us
  matrix products: 31.5 us -> 0 us
  other arithmetic: 13.5 us -> 0 us
  between operations: 13.9 us -> 0.64 us
  starting transfers between devices: 6.81 us -> 0 us
    all_gather x4 -> x0, waiting for transfers between devices: 232 us -> none  [the longest x1 117 us: local(): lax.all_gather(text_features, COL, axis=1, tiled=True)]
    pallas_call x0 -> x1, Pallas kernels: none -> 120 us  [local(): pl.pallas_call(kernel, out_shape=(jax.ShapeDtypeStruct((HALF, LA * LB), F...]
    dot_general x3 -> x0, matrix products: 31.5 us -> none  [the longest x1 14.1 us: local(): jnp.einsum('lrd,lcd->lrc', text_block, text_set, preferred_element_type=j...]
    psum x4 -> x0, blocking collectives: 28.9 us -> none  [by_axis(): return functools.reduce(lax.psum, axes, shard)]
    all_to_all x1 -> x0, blocking collectives: 25.5 us -> none  [from_everyone(): return lax.all_to_all(copies, axis, split_axis=0, concat_axis=0, tiled=True)]
    reduce_sum x4 -> x0, other arithmetic: 12 us -> none  [the longest x1 7.18 us: local(): jnp.sum(text_block.astype(jnp.float32), axis=1)]
    all_to_all x1 -> x0, starting transfers between devices: 6.66 us -> none  [summed_on_arrival(): lax.all_to_all(cut_along(shard, dim, devices), axis, 0, 0, tiled=True)]
  transfers between devices with their start and end apart: 5 -> 0, of which waited for: 4 -> 0; matrix products, arithmetic and copies ran while one was open for 6% -> 0% of each run, Pallas kernels for 0% -> 0%
where the time goes in v1:
time: 123 us
  Pallas kernels  120 us (98%)
  local copies, waits for them, and re-layouts  2.59 us (2%)
    pallas_call x1, Pallas kernels, local(): pl.pallas_call(kernel, out_shape=(jax.ShapeDtypeStruct((HALF, LA * LB), F...  120 us
    unnamed x2, local copies, waits for them, and re-layouts  2.59 us

profile of v1, /device:TPU:1, one launch (start us, length us, event | category | flops | bytes accessed | tf_op | source)
XLA Modules:
  0.0 123.2 jit_solution(4272951710295333601)
XLA Ops:
  0.6 120.0 %shard_map.41 = (f32[32,30]{1,0:T(8,128)}, f32[5,6]{1,0:T(8,128)}) custom-call(bf16[5,32,3584]{2,1,0:T(8,128)(2,1)} %text.1, bf16[6,32,1024]{2,1,0:T(8,128)(2,1)} %vision.1), custom_call_target="tpu_custom_call" | custom-call | tf_op jit(solution)/shard_map/pallas_call | solution.py:343
  120.6 1.3 %copy.6 = f32[32,30]{1,0:T(8,128)} copy(f32[32,30]{1,0:T(8,128)} %get-tuple-element.4) | data formatting | bytes 7680
  121.9 1.3 %copy.7 = f32[5,6]{1,0:T(8,128)} copy(f32[5,6]{1,0:T(8,128)} %get-tuple-element.5) | data formatting | bytes 240

commit v2 on v1

--- a/solution.py
+++ b/solution.py
@@ -20,10 +20,11 @@
     ((10, 1, 5), (2, 3, 1), (11, 4, 0), (0, 6, 4)),
     ((6, 5, 0), (1, 7, 2), (3, 9, 3)),
 )
-CHUNKS, WIDTH = 24, 512
+CHUNKS, WIDTH = 48, 256
+PAIRS = CHUNKS // 2
 ROWS, HALF = 64, 32
 ALL = len(BLOCKS) * ROWS
-AHEAD, LAG, LATE = 3, 2, 2
+EARLY, LAG, LATE, PACE = 4, 5, 3, 5
 LAST = (3, 10, 17, 19, 21, 23)
 F32, BF16 = jnp.float32, jnp.bfloat16
 MESH = pl.DeviceIdType.MESH
@@ -31,7 +32,7 @@
 
 def kernel(
     text, vision, terms, cka,
-    buf, acc, rx, xc, sums, mrx, rs, selfs, rrx, row, ar1, ar2,
+    buf, acc, rx, xc, sums, mrx, rs, selfs, pack, rrx, row, ar1, ar2,
     load_sem, swap_send, swap_recv, mean_send, mean_recv, hop_send, hop_recv,
     ex_send, ex_recv, rs_send, rs_recv, ar1_send, ar1_recv, ar2_send, ar2_recv,
 ):
@@ -54,14 +55,15 @@
     here = (0, 0, 0)
 
     def source(c, core):
-        if c < 4:
+        if c < 8:
             return text.at[2, :, pl.ds(pl.multiple_of(core * 1536 + c * WIDTH, WIDTH), WIDTH)]
-        if c < 11:
-            return text.at[core * 3, :, pl.ds((c - 4) * WIDTH, WIDTH)]
-        if c < 18:
-            return text.at[core * 3 + 1, :, pl.ds((c - 11) * WIDTH, WIDTH)]
-        return vision.at[core * 3 + (c - 18) // 2, :, pl.ds((c - 18) % 2 * WIDTH, WIDTH)]
-
+        if c < 22:
+            return text.at[core * 3, :, pl.ds((c - 8) * WIDTH, WIDTH)]
+        if c < 36:
+            return text.at[core * 3 + 1, :, pl.ds((c - 22) * WIDTH, WIDTH)]
+        return vision.at[core * 3 + (c - 36) // 4, :, pl.ds((c - 36) % 4 * WIDTH, WIDTH)]
+
+    first = 2 * p
     mine = pl.ds(pl.multiple_of(OWN * ROWS + p * HALF, HALF), HALF)
 
     def load(c):
@@ -71,11 +73,22 @@
         return remote(source(c, other), buf.at[c, mine, :], swap_send.at[c], swap_recv.at[c], at(here, other))
 
     for c in range(CHUNKS):
-        if c == 0:
-            pl.when(p == 0)(lambda: load(0).start())
-            pl.when(p == 1)(lambda: swap(0).start())
+        if c < 2:
+            pl.when(p == 0)(lambda c=c: load(c).start())
         else:
             load(c).start()
+
+    barrier = pltpu.get_barrier_semaphore()
+    greeted = [at(step, p) for step in STEPS]
+    greeted.append(at(here, other))
+    for device in greeted:
+        pl.semaphore_signal(barrier, inc=1, device_id=device, device_id_type=MESH)
+    pl.semaphore_wait(barrier, len(greeted))
+
+    for c in range(CHUNKS):
+        if c < 2:
+            pl.when(p == 1)(lambda c=c: swap(c).start())
+        else:
             swap(c).start()
 
     @pl.loop(0, 36)
@@ -84,17 +97,6 @@
 
     rs[...] = jnp.zeros_like(rs)
     selfs[...] = jnp.zeros_like(selfs)
-
-    sums[0, 0:1, :] = jnp.zeros((1, WIDTH), F32)
-    ones = jnp.ones((8, ROWS), BF16)
-
-    @pl.loop(p, CHUNKS)
-    def _(c):
-        part = buf.at[c, mine, :]
-        pltpu.make_async_copy(part, part, load_sem.at[c]).wait()
-        pltpu.make_async_copy(part, part, swap_recv.at[c]).wait()
-        total = jnp.dot(ones, buf[c, OWN * ROWS : (OWN + 1) * ROWS, :], preferred_element_type=F32)
-        sums[0, pl.ds(c, 1), :] = total[0:1]
 
     def hop(edge, c):
         held, becomes, step = edge
@@ -102,49 +104,41 @@
             buf.at[c, pl.ds(held * ROWS, ROWS), :],
             buf.at[c, pl.ds(becomes * ROWS, ROWS), :],
             hop_send.at[c],
-            hop_recv.at[c, becomes],
+            hop_recv.at[c, kind[becomes]],
             at(back(STEPS[step]), p),
         )
 
-    def arrived(block, c):
-        part = buf.at[c, pl.ds(block * ROWS, ROWS), :]
-        pltpu.make_async_copy(part, part, hop_recv.at[c, block]).wait()
+    inner = [sorted({e[0] for e in EDGES[d]}) for d in range(3)]
+    kind = {e[1]: next((d - 1 for d in (1, 2) if e[1] in inner[d]), 2) for d in EDGES for e in d}
+
+    def arrived(which, c):
+        part = buf.at[c, pl.ds(0, ROWS * sum(k == which for k in kind.values())), :]
+        pltpu.make_async_copy(part, part, hop_recv.at[c, which]).wait()
 
     def send_own(c):
         for edge in EDGES[0]:
             hop(edge, c).start()
 
-    def mean_copy(axis, k):
-        offset = tuple(k if i == axis else 0 for i in range(3))
-        return remote(
-            sums.at[axis], mrx.at[axis, k - 1], mean_send.at[axis, k - 1], mean_recv.at[axis, k - 1], at(offset, p)
-        )
-
-    for axis in range(3):
-        for k in (1, 2, 3):
-            mean_copy(axis, k).start()
-        if axis == 0:
-            pl.when(p == 0)(lambda: send_own(0))
-        else:
-            send_own(axis)
-        for k in (1, 2, 3):
-            mean_copy(axis, k).wait_recv()
-        sums[axis + 1] = (sums[axis] + mrx[axis, 0]) + (mrx[axis, 1] + mrx[axis, 2])
-
-    inner = [sorted({e[0] for e in EDGES[d]}) for d in range(3)]
-    leaves = [e[1] for d in EDGES for e in d if all(e[1] not in s for s in inner)]
+    where = (x, y, z)
+
+    def mean_copy(n):
+        axis, second = n // 2, n % 2
+        place = list(where)
+        place[axis] = 3 - where[axis] if second else where[axis] + 1 - 2 * lax.rem(where[axis], 2)
+        device = (place[1], p, place[2], place[0])
+        return remote(sums.at[n], mrx.at[n], mean_send.at[n], mean_recv.at[n], device)
 
     def exchange(layer):
         return remote(
             acc.at[layer, pl.ds(other * 3, 3)], rx.at[layer], ex_send.at[layer], ex_recv.at[layer], at(here, other)
         )
 
-    def compute(c):
-        for block in leaves:
-            arrived(block, c)
-        mean = sums[3, pl.ds(c, 1), :] * (1.0 / STIMULI)
-        xc[...] = (buf[c].astype(F32) - mean).astype(BF16)
-        layer = jnp.where(c < 4, 0, jnp.where(c < 11, 1, jnp.where(c < 18, 2, 3 + (c - 18) // 2)))
+    def compute(k):
+        for h in range(2):
+            arrived(2, 2 * k + h)
+            mean = sums[6, pl.ds(2 * k + h, 1), :] * (1.0 / STIMULI)
+            xc[:, h * WIDTH : (h + 1) * WIDTH] = (buf[2 * k + h].astype(F32) - mean).astype(BF16)
+        layer = jnp.where(k < 4, 0, jnp.where(k < 11, 1, jnp.where(k < 18, 2, 3 + (k - 18) // 2)))
         for g in range(3):
             tile = lax.dot_general(
                 xc[...],
@@ -155,32 +149,65 @@
             acc[layer, 2 * g] += tile[:, :128]
             acc[layer, 2 * g + 1] += tile[:, 128:]
         for layer, last in enumerate(LAST):
-            pl.when(c == last)(lambda layer=layer: exchange(layer).start())
-
-    @pl.loop(min(AHEAD, LAG), CHUNKS + 2 * LAG + LATE)
+            pl.when(k == last)(lambda layer=layer: exchange(layer).start())
+
+    def computed(u):
+        ready = jnp.minimum((u - LAG - LATE + 1) // 2, u - (6 * PACE - 1))
+        return jnp.minimum(jnp.maximum(ready, p), PAIRS)
+
+    def here_now(c):
+        part = buf.at[c, mine, :]
+        pltpu.make_async_copy(part, part, load_sem.at[c]).wait()
+        pltpu.make_async_copy(part, part, swap_recv.at[c]).wait()
+
+    @pl.loop(first, EARLY)
+    def _(c):
+        here_now(c)
+        send_own(c)
+
+    @pl.loop(EARLY, CHUNKS)
+    def _(c):
+        here_now(c)
+
+    for c in range(CHUNKS):
+        total = jnp.sum(buf[c, OWN * ROWS : (OWN + 1) * ROWS, :].astype(F32), axis=0, keepdims=True)
+        sums[0, c : c + 1, :] = jnp.where(p == 1, 0.0, total) if c < 2 else total
+
+    mean_copy(0).start()
+
+    @pl.loop(0, CHUNKS + LAG + LATE)
     def _(u):
-        @pl.when((u >= AHEAD) & (u < CHUNKS))
+        for n in range(1, 6):
+            pl.when(u == PACE * n)(lambda n=n: mean_copy(n).start())
+
+        @pl.when(u + EARLY < CHUNKS)
         def _():
-            send_own(u)
+            send_own(u + EARLY)
 
         for depth in (1, 2):
-            c = u - depth * LAG
-
-            @pl.when((c >= p) & (c < CHUNKS))
+            c = u - (depth - 1) * LAG
+
+            @pl.when((c >= first) & (c < CHUNKS))
             def _():
-                for block in inner[depth]:
-                    arrived(block, c)
+                arrived(depth - 1, c)
                 for edge in EDGES[depth]:
                     hop(edge, c).start()
 
-        c = u - 2 * LAG - LATE
-
-        @pl.when((c >= p) & (c < CHUNKS))
-        def _():
-            compute(c)
+        for n in range(6):
+
+            @pl.when(u == PACE * n + PACE - 1)
+            def _():
+                mean_copy(n).wait_recv()
+                sums[n + 1] = sums[n] + mrx[n]
+
+        @pl.loop(computed(u - 1), computed(u))
+        def _(k):
+            compute(k)
 
     for layer in range(6):
         exchange(layer).wait_recv()
+
+    lanes8 = lax.broadcasted_iota(jnp.int32, (8, 128), 1)
 
     def products(core):
         texts = (0, 1, 2, 3, 4) if core == 0 else (3, 4, 2, 0, 1)
@@ -226,13 +253,24 @@
 
             for j in (2 * q, 2 * q + 1):
                 for to in (0, 1):
+                    first = j % 2 * ROWS + to * HALF
+                    tile = jnp.zeros((8, 128), F32)
+                    for g in range(4):
+                        turned = rs[i, 8 * g : 8 * g + 8, :]
+                        if (g * HALF - first) % 128:
+                            turned = pltpu.roll(turned, (g * HALF - first) % 128, 1)
+                        tile = jnp.where(lanes8 // HALF == g, turned, tile)
                     if j == OWN and to == core:
-                        rrx[j] = rs[i]
+                        rrx[j] = tile
                     else:
+                        pack[i, j % 2, to] = tile
+            for j in (2 * q, 2 * q + 1):
+                for to in (0, 1):
+                    if not (j == OWN and to == core):
                         share(i, j, to).start()
 
     def share(i, j, to):
-        return remote(rs.at[i], rrx.at[j], rs_send.at[i, j % 2, to], rs_recv.at[j], at(BLOCKS[j], to))
+        return remote(pack.at[i, j % 2, to], rrx.at[j], rs_send.at[i, j % 2, to], rs_recv.at[j], at(BLOCKS[j], to))
 
     for core in (0, 1):
         pl.when(p == core)(lambda core=core: products(core))
@@ -288,10 +326,9 @@
             pl.when(p != OWN // 6)(lambda: pltpu.make_async_copy(rrx.at[OWN], rrx.at[OWN], rs_recv.at[OWN]).wait())
         else:
             pltpu.make_async_copy(rrx.at[j], rrx.at[j], rs_recv.at[j]).wait()
-    even = ((rrx[0] + rrx[2]) + (rrx[4] + rrx[6])) + (rrx[8] + rrx[10])
-    odd = ((rrx[1] + rrx[3]) + (rrx[5] + rrx[7])) + (rrx[9] + rrx[11])
-    share_sum = even + pltpu.roll(odd, 64, 1)
-    share_sum = jnp.where(p == 0, share_sum, pltpu.roll(share_sum, 96, 1))
+    packed = ((rrx[0] + rrx[1]) + (rrx[2] + rrx[3])) + ((rrx[4] + rrx[5]) + (rrx[6] + rrx[7]))
+    packed += (rrx[8] + rrx[9]) + (rrx[10] + rrx[11])
+    share_sum = jnp.concatenate([packed] + [pltpu.roll(packed, 128 - g * HALF, 1) for g in (1, 2, 3)], axis=0)
     out = jnp.transpose(share_sum * (scale * STIMULI))
     terms[...] = out[:HALF, : LA * LB]
 
@@ -306,15 +343,14 @@
     cka[...] = ratio
 
     for c in range(CHUNKS):
-        if c == 0:
-            pl.when(p == 1)(lambda: swap(0).wait_send())
+        if c < 2:
+            pl.when(p == 1)(lambda c=c: swap(c).wait_send())
         else:
             swap(c).wait_send()
-    for axis in range(3):
-        for k in (1, 2, 3):
-            mean_copy(axis, k).wait_send()
-
-    @pl.loop(p, CHUNKS)
+    for n in range(6):
+        mean_copy(n).wait_send()
+
+    @pl.loop(first, CHUNKS)
     def _(c):
         part = buf.at[c, pl.ds(0, ALL - ROWS), :]
         pltpu.make_async_copy(part, part, hop_send.at[c]).wait()
@@ -352,22 +388,23 @@
             pltpu.VMEM((CHUNKS, ALL, WIDTH), BF16),
             pltpu.VMEM((6, 6, ALL, 128), F32),
             pltpu.VMEM((6, 3, ALL, 128), F32),
-            pltpu.VMEM((ALL, WIDTH), BF16),
-            pltpu.VMEM((4, CHUNKS, WIDTH), F32),
-            pltpu.VMEM((3, 3, CHUNKS, WIDTH), F32),
+            pltpu.VMEM((ALL, 2 * WIDTH), BF16),
+            pltpu.VMEM((7, CHUNKS, WIDTH), F32),
+            pltpu.VMEM((6, CHUNKS, WIDTH), F32),
             pltpu.VMEM((3, 32, 128), F32),
             pltpu.VMEM((16, 128), F32),
-            pltpu.VMEM((12, 32, 128), F32),
+            pltpu.VMEM((3, 2, 2, 8, 128), F32),
+            pltpu.VMEM((12, 8, 128), F32),
             pltpu.VMEM((2, 1, 128), F32),
             pltpu.VMEM((16, 1, 128), F32),
             pltpu.VMEM((8, 1, 128), F32),
             dma((CHUNKS,)),
             dma((CHUNKS,)),
             dma((CHUNKS,)),
-            dma((3, 3)),
-            dma((3, 3)),
+            dma((6,)),
+            dma((6,)),
             dma((CHUNKS,)),
-            dma((CHUNKS, len(BLOCKS))),
+            dma((CHUNKS, 3)),
             dma((6,)),
             dma((6,)),
             dma((3, 2, 2)),
@@ -377,7 +414,7 @@
             dma((7,)),
             dma((8,)),
         ],
-        compiler_params=pltpu.CompilerParams(has_side_effects=True, vmem_limit_bytes=60 * 2**20),
+        compiler_params=pltpu.CompilerParams(collective_id=0, has_side_effects=True, vmem_limit_bytes=60 * 2**20),
     )(text_features, vision_features)
 
 

time: 123 us -> 107 us (0.87)
  Pallas kernels: 120 us -> 104 us
    pallas_call x1, Pallas kernels: 120 us -> 104 us  [local(): pl.pallas_call(kernel, out_shape=(jax.ShapeDtypeStruct((HALF, LA * LB), F...]
where the time goes in v2:
time: 107 us
  Pallas kernels  104 us (97%)
  local copies, waits for them, and re-layouts  2.59 us (2%)
    pallas_call x1, Pallas kernels, local(): pl.pallas_call(kernel, out_shape=(jax.ShapeDtypeStruct((HALF, LA * LB), F...  104 us
    unnamed x2, local copies, waits for them, and re-layouts  2.59 us

profile of v2, /device:TPU:1, one launch (start us, length us, event | category | flops | bytes accessed | tf_op | source)
XLA Modules:
  0.0 106.8 jit_solution(9177404642825274350)
XLA Ops:
  0.6 103.5 %shard_map.41 = (f32[32,30]{1,0:T(8,128)}, f32[5,6]{1,0:T(8,128)}) custom-call(bf16[5,32,3584]{2,1,0:T(8,128)(2,1)} %text.1, bf16[6,32,1024]{2,1,0:T(8,128)(2,1)} %vision.1), custom_call_target="tpu_custom_call" | custom-call | tf_op jit(solution)/shard_map/pallas_call | solution.py:379
  104.2 1.3 %copy.6 = f32[32,30]{1,0:T(8,128)} copy(f32[32,30]{1,0:T(8,128)} %get-tuple-element.4) | data formatting | bytes 7680
  105.5 1.3 %copy.7 = f32[5,6]{1,0:T(8,128)} copy(f32[5,6]{1,0:T(8,128)} %get-tuple-element.5) | data formatting | bytes 240

commit v3 on v2

--- a/solution.py
+++ b/solution.py
@@ -24,14 +24,14 @@
 PAIRS = CHUNKS // 2
 ROWS, HALF = 64, 32
 ALL = len(BLOCKS) * ROWS
-EARLY, LAG, LATE, PACE = 4, 5, 3, 5
+EARLY, LAG, LATE, PACE = 4, 4, 3, 4
 LAST = (3, 10, 17, 19, 21, 23)
 F32, BF16 = jnp.float32, jnp.bfloat16
 MESH = pl.DeviceIdType.MESH
 
 
 def kernel(
-    text, vision, terms, cka,
+    text, vision, raw,
     buf, acc, rx, xc, sums, mrx, rs, selfs, pack, rrx, row, ar1, ar2,
     load_sem, swap_send, swap_recv, mean_send, mean_recv, hop_send, hop_recv,
     ex_send, ex_recv, rs_send, rs_recv, ar1_send, ar1_recv, ar2_send, ar2_recv,
@@ -129,9 +129,66 @@
         return remote(sums.at[n], mrx.at[n], mean_send.at[n], mean_recv.at[n], device)
 
     def exchange(layer):
-        return remote(
-            acc.at[layer, pl.ds(other * 3, 3)], rx.at[layer], ex_send.at[layer], ex_recv.at[layer], at(here, other)
-        )
+        for core in (0, 1):
+
+            @pl.when(p == core)
+            def _():
+                for i in range(3):
+                    q = (1 - core) * 3 + i
+                    for block in STRIPS[q]:
+                        strip = pl.ds(block * ROWS, ROWS)
+                        remote(
+                            acc.at[layer, q, strip],
+                            rx.at[layer, i, strip],
+                            ex_send.at[layer],
+                            ex_recv.at[layer],
+                            at(here, other),
+                        ).start()
+
+    def exchanged(sem):
+        part = acc.at[0, pl.ds(0, 2), pl.ds(0, 8 * ROWS)]
+        pltpu.make_async_copy(part, part, sem).wait()
+
+    def products(core, k):
+        texts = (0, 1, 2, 3, 4) if core == 0 else (3, 4, 2, 0, 1)
+        for i in range(3):
+            q = core * 3 + i
+            n_text = LA if k == 0 else 0
+
+            def body(r, sums_):
+                s = list(sums_)
+                for block in STRIPS[q]:
+                    at_ = pl.ds(pl.multiple_of(block * ROWS + r * 8, 8), 8)
+                    t = (
+                        acc[1, q, at_, :],
+                        acc[2, q, at_, :],
+                        acc[0, q, at_, :] + rx[0, i, at_, :],
+                        rx[1, i, at_, :],
+                        rx[2, i, at_, :],
+                    )
+                    v = (acc[3 + k, q, at_, :], rx[3 + k, i, at_, :])
+                    for a in range(LA):
+                        for b in range(2):
+                            s[2 * a + b] += t[a] * v[b]
+                    for b in range(2):
+                        s[10 + b] += v[b] * v[b]
+                    for a in range(n_text):
+                        s[12 + a] += t[a] * t[a]
+                return tuple(s)
+
+            zero = jnp.zeros((8, 128), F32)
+            s = lax.fori_loop(0, 8, body, (zero,) * (12 + n_text))
+            visions = (core * 3 + k, (1 - core) * 3 + k)
+            for a in range(LA):
+                for b in range(2):
+                    n = texts[a] * LB + visions[b]
+                    rs[i, n : n + 1, :] = jnp.sum(s[2 * a + b], axis=0, keepdims=True)
+            for b in range(2):
+                n = 8 + visions[b]
+                selfs[n : n + 1, :] += jnp.sum(s[10 + b], axis=0, keepdims=True)
+            for a in range(n_text):
+                n = texts[a]
+                selfs[n : n + 1, :] += jnp.sum(s[12 + a], axis=0, keepdims=True)
 
     def compute(k):
         for h in range(2):
@@ -140,16 +197,29 @@
             xc[:, h * WIDTH : (h + 1) * WIDTH] = (buf[2 * k + h].astype(F32) - mean).astype(BF16)
         layer = jnp.where(k < 4, 0, jnp.where(k < 11, 1, jnp.where(k < 18, 2, 3 + (k - 18) // 2)))
         for g in range(3):
+            blocks = sorted({*STRIPS[2 * g], *STRIPS[2 * g + 1]})
             tile = lax.dot_general(
-                xc[...],
+                jnp.concatenate([xc[b * ROWS : (b + 1) * ROWS, :] for b in blocks], axis=0),
                 xc[g * 256 : (g + 1) * 256, :],
                 (((1,), (1,)), ((), ())),
                 preferred_element_type=F32,
             )
-            acc[layer, 2 * g] += tile[:, :128]
-            acc[layer, 2 * g + 1] += tile[:, 128:]
+            for n, b in enumerate(blocks):
+                strip = slice(b * ROWS, (b + 1) * ROWS)
+                for h in range(2):
+                    if b in STRIPS[2 * g + h]:
+                        acc[layer, 2 * g + h, strip] += tile[n * ROWS : (n + 1) * ROWS, h * 128 : (h + 1) * 128]
         for layer, last in enumerate(LAST):
-            pl.when(k == last)(lambda layer=layer: exchange(layer).start())
+            pl.when(k == last)(lambda layer=layer: exchange(layer))
+        for n in (0, 1):
+
+            @pl.when(k == LAST[3 + n] + 1)
+            def _():
+                for layer in (0, 1, 2, 3) if n == 0 else (4,):
+                    exchanged(ex_recv.at[layer])
+                for core in (0, 1):
+                    pl.when(p == core)(lambda core=core: products(core, n))
+
 
     def computed(u):
         ready = jnp.minimum((u - LAG - LATE + 1) // 2, u - (6 * PACE - 1))
@@ -160,10 +230,28 @@
         pltpu.make_async_copy(part, part, load_sem.at[c]).wait()
         pltpu.make_async_copy(part, part, swap_recv.at[c]).wait()
 
+    def send_half(c, core):
+        for held, becomes, step in EDGES[0]:
+            rows = [pl.ds(pl.multiple_of(b * ROWS + core * HALF, HALF), HALF) for b in (held, becomes)]
+            remote(
+                buf.at[c, rows[0], :],
+                buf.at[c, rows[1], :],
+                hop_send.at[c],
+                hop_recv.at[c, kind[becomes]],
+                at(back(STEPS[step]), p),
+            ).start()
+
     @pl.loop(first, EARLY)
     def _(c):
-        here_now(c)
-        send_own(c)
+        part = buf.at[c, mine, :]
+        pltpu.make_async_copy(part, part, load_sem.at[c]).wait()
+        send_half(c, p)
+
+    @pl.loop(first, EARLY)
+    def _(c):
+        part = buf.at[c, mine, :]
+        pltpu.make_async_copy(part, part, swap_recv.at[c]).wait()
+        send_half(c, other)
 
     @pl.loop(EARLY, CHUNKS)
     def _(c):
@@ -204,53 +292,13 @@
         def _(k):
             compute(k)
 
-    for layer in range(6):
-        exchange(layer).wait_recv()
+    exchanged(ex_recv.at[5])
 
     lanes8 = lax.broadcasted_iota(jnp.int32, (8, 128), 1)
 
-    def products(core):
-        texts = (0, 1, 2, 3, 4) if core == 0 else (3, 4, 2, 0, 1)
+    def deliver(core):
         for i in range(3):
             q = core * 3 + i
-            for k in range(3):
-                n_text = LA if k == 0 else 0
-
-                def body(r, sums_):
-                    s = list(sums_)
-                    for block in STRIPS[q]:
-                        at_ = pl.ds(pl.multiple_of(block * ROWS + r * 8, 8), 8)
-                        t = (
-                            acc[1, q, at_, :],
-                            acc[2, q, at_, :],
-                            acc[0, q, at_, :] + rx[0, i, at_, :],
-                            rx[1, i, at_, :],
-                            rx[2, i, at_, :],
-                        )
-                        v = (acc[3 + k, q, at_, :], rx[3 + k, i, at_, :])
-                        for a in range(LA):
-                            for b in range(2):
-                                s[2 * a + b] += t[a] * v[b]
-                        for b in range(2):
-                            s[10 + b] += v[b] * v[b]
-                        for a in range(n_text):
-                            s[12 + a] += t[a] * t[a]
-                    return tuple(s)
-
-                zero = jnp.zeros((8, 128), F32)
-                s = lax.fori_loop(0, 8, body, (zero,) * (12 + n_text))
-                visions = (core * 3 + k, (1 - core) * 3 + k)
-                for a in range(LA):
-                    for b in range(2):
-                        n = texts[a] * LB + visions[b]
-                        rs[i, n : n + 1, :] = jnp.sum(s[2 * a + b], axis=0, keepdims=True)
-                for b in range(2):
-                    n = 8 + visions[b]
-                    selfs[n : n + 1, :] += jnp.sum(s[10 + b], axis=0, keepdims=True)
-                for a in range(n_text):
-                    n = texts[a]
-                    selfs[n : n + 1, :] += jnp.sum(s[12 + a], axis=0, keepdims=True)
-
             for j in (2 * q, 2 * q + 1):
                 for to in (0, 1):
                     first = j % 2 * ROWS + to * HALF
@@ -273,7 +321,10 @@
         return remote(pack.at[i, j % 2, to], rrx.at[j], rs_send.at[i, j % 2, to], rs_recv.at[j], at(BLOCKS[j], to))
 
     for core in (0, 1):
-        pl.when(p == core)(lambda core=core: products(core))
+
+        @pl.when(p == core)
+        def _():
+            products(core, 2)
 
     cross = rs[0] + rs[1] + rs[2]
     parts = jnp.concatenate([cross, selfs[...]], axis=0)
@@ -291,6 +342,8 @@
 
     for n in range(15):
         over_plane(n).start()
+    for core in (0, 1):
+        pl.when(p == core)(lambda core=core: deliver(core))
     ar1[me1] = row[0]
     for dx, dy in plane:
         n = lax.rem(x + dx, 4) * 4 + lax.rem(y + dy, 4)
@@ -329,8 +382,7 @@
     packed = ((rrx[0] + rrx[1]) + (rrx[2] + rrx[3])) + ((rrx[4] + rrx[5]) + (rrx[6] + rrx[7]))
     packed += (rrx[8] + rrx[9]) + (rrx[10] + rrx[11])
     share_sum = jnp.concatenate([packed] + [pltpu.roll(packed, 128 - g * HALF, 1) for g in (1, 2, 3)], axis=0)
-    out = jnp.transpose(share_sum * (scale * STIMULI))
-    terms[...] = out[:HALF, : LA * LB]
+    raw[0:32] = share_sum * (scale * STIMULI)
 
     a_sub = lax.broadcasted_iota(jnp.int32, (8, 1), 0)
     spread = jnp.broadcast_to(total, (8, 128))
@@ -339,8 +391,7 @@
         crosses = jnp.where(a_sub == a, pltpu.roll(spread, 128 - a * LB, 1), crosses)
     text_self = pick(32 + jnp.minimum(a_sub, LA - 1), 8)
     vision_self = pltpu.roll(spread, 128 - 40, 1)
-    ratio = crosses[:LA, :LB] * (1.0 / jnp.sqrt(text_self[:LA] * vision_self[:LA, :LB]))
-    cka[...] = ratio
+    raw[32:37, :LB] = crosses[:LA, :LB] * (1.0 / jnp.sqrt(text_self[:LA] * vision_self[:LA, :LB]))
 
     for c in range(CHUNKS):
         if c < 2:
@@ -356,7 +407,7 @@
         pltpu.make_async_copy(part, part, hop_send.at[c]).wait()
 
     for layer in range(6):
-        exchange(layer).wait_send()
+        exchanged(ex_send.at[layer])
 
     def drain(core):
         for i in range(3):
@@ -374,16 +425,18 @@
         over_column(n).wait_send()
 
 
+def write(raw, terms, cka):
+    terms[...] = jnp.transpose(raw[0:32])[:HALF, : LA * LB]
+    cka[...] = raw[32:37, :LB]
+
+
 def local(text_features, vision_features):
     dma = pltpu.SemaphoreType.DMA
-    return pl.pallas_call(
+    raw = pl.pallas_call(
         kernel,
-        out_shape=(
-            jax.ShapeDtypeStruct((HALF, LA * LB), F32),
-            jax.ShapeDtypeStruct((LA, LB), F32),
-        ),
+        out_shape=jax.ShapeDtypeStruct((40, 128), F32),
         in_specs=[pl.BlockSpec(memory_space=pl.ANY)] * 2,
-        out_specs=(pl.BlockSpec(memory_space=pltpu.VMEM), pl.BlockSpec(memory_space=pltpu.VMEM)),
+        out_specs=pl.BlockSpec(memory_space=pltpu.VMEM),
         scratch_shapes=[
             pltpu.VMEM((CHUNKS, ALL, WIDTH), BF16),
             pltpu.VMEM((6, 6, ALL, 128), F32),
@@ -416,6 +469,15 @@
         ],
         compiler_params=pltpu.CompilerParams(collective_id=0, has_side_effects=True, vmem_limit_bytes=60 * 2**20),
     )(text_features, vision_features)
+    return pl.pallas_call(
+        write,
+        out_shape=(
+            jax.ShapeDtypeStruct((HALF, LA * LB), F32),
+            jax.ShapeDtypeStruct((LA, LB), F32),
+        ),
+        in_specs=[pl.BlockSpec(memory_space=pltpu.VMEM)],
+        out_specs=(pl.BlockSpec(memory_space=pltpu.VMEM),) * 2,
+    )(raw)
 
 
 def solution(mesh):

time: 107 us -> 103 us (0.963)
  local copies, waits for them, and re-layouts: 2.59 us -> 0 us
  Pallas kernels: 104 us -> 102 us
    unnamed x2 -> x0, local copies, waits for them, and re-layouts: 2.59 us -> none
    pallas_call x1 -> x2, Pallas kernels: 104 us -> 102 us  [the longest x1 101 us: local(): pl.pallas_call(kernel, out_shape=jax.ShapeDtypeStruct((40, 128), F32), in...]
where the time goes in v3:
time: 103 us
  Pallas kernels  102 us (99%)
    pallas_call x1, Pallas kernels, local(): pl.pallas_call(kernel, out_shape=jax.ShapeDtypeStruct((40, 128), F32), in...  101 us

profile of v3, /device:TPU:1, one launch (start us, length us, event | category | flops | bytes accessed | tf_op | source)
XLA Modules:
  0.0 103.0 jit_solution(11471263023048520339)
XLA Ops:
  0.6 100.9 %shard_map.41.raw = f32[40,128]{1,0:T(8,128)} custom-call(bf16[5,32,3584]{2,1,0:T(8,128)(2,1)} %text.1, bf16[6,32,1024]{2,1,0:T(8,128)(2,1)} %vision.1), custom_call_target="tpu_custom_call" | custom-call | tf_op jit(solution)/shard_map/pallas_call | solution.py:435
  101.6 1.4 %shard_map.42 = (f32[32,30]{1,0:T(8,128)}, f32[5,6]{1,0:T(8,128)}) custom-call(f32[40,128]{1,0:T(8,128)} %shard_map.41.raw), custom_call_target="tpu_custom_call" | custom-call | tf_op jit(solution)/shard_map/pallas_call | solution.py:472

commit v4 on v3

--- a/solution.py
+++ b/solution.py
@@ -33,7 +33,7 @@
 def kernel(
     text, vision, raw,
     buf, acc, rx, xc, sums, mrx, rs, selfs, pack, rrx, row, ar1, ar2,
-    load_sem, swap_send, swap_recv, mean_send, mean_recv, hop_send, hop_recv,
+    load_sem, swap_send, swap_recv, mean_send, mean_recv, hop_send, hop_recv, last_recv,
     ex_send, ex_recv, rs_send, rs_recv, ar1_send, ar1_recv, ar2_send, ar2_recv,
 ):
     y, p = lax.axis_index("row_0"), lax.axis_index("row_1")
@@ -67,10 +67,10 @@
     mine = pl.ds(pl.multiple_of(OWN * ROWS + p * HALF, HALF), HALF)
 
     def load(c):
-        return pltpu.make_async_copy(source(c, p), buf.at[c, mine, :], load_sem.at[c])
+        return pltpu.make_async_copy(source(c, p), buf.at[c, mine, :], load_sem.at[min(c, EARLY)])
 
     def swap(c):
-        return remote(source(c, other), buf.at[c, mine, :], swap_send.at[c], swap_recv.at[c], at(here, other))
+        return remote(source(c, other), buf.at[c, mine, :], swap_send, swap_recv.at[min(c, EARLY)], at(here, other))
 
     for c in range(CHUNKS):
         if c < 2:
@@ -103,8 +103,8 @@
         return remote(
             buf.at[c, pl.ds(held * ROWS, ROWS), :],
             buf.at[c, pl.ds(becomes * ROWS, ROWS), :],
-            hop_send.at[c],
-            hop_recv.at[c, kind[becomes]],
+            hop_send,
+            last_recv.at[c // 2] if kind[becomes] == 2 else hop_recv.at[kind[becomes], c],
             at(back(STEPS[step]), p),
         )
 
@@ -113,7 +113,11 @@
 
     def arrived(which, c):
         part = buf.at[c, pl.ds(0, ROWS * sum(k == which for k in kind.values())), :]
-        pltpu.make_async_copy(part, part, hop_recv.at[c, which]).wait()
+        pltpu.make_async_copy(part, part, hop_recv.at[which, c]).wait()
+
+    def arrived_pair(k):
+        part = buf.at[pl.ds(2 * k, 2), pl.ds(0, ROWS * sum(k == 2 for k in kind.values())), :]
+        pltpu.make_async_copy(part, part, last_recv.at[k]).wait()
 
     def send_own(c):
         for edge in EDGES[0]:
@@ -126,7 +130,7 @@
         place = list(where)
         place[axis] = 3 - where[axis] if second else where[axis] + 1 - 2 * lax.rem(where[axis], 2)
         device = (place[1], p, place[2], place[0])
-        return remote(sums.at[n], mrx.at[n], mean_send.at[n], mean_recv.at[n], device)
+        return remote(sums.at[n], mrx.at[n], mean_send, mean_recv.at[n], device)
 
     def exchange(layer):
         for core in (0, 1):
@@ -140,7 +144,7 @@
                         remote(
                             acc.at[layer, q, strip],
                             rx.at[layer, i, strip],
-                            ex_send.at[layer],
+                            ex_send,
                             ex_recv.at[layer],
                             at(here, other),
                         ).start()
@@ -191,8 +195,8 @@
                 selfs[n : n + 1, :] += jnp.sum(s[12 + a], axis=0, keepdims=True)
 
     def compute(k):
+        arrived_pair(k)
         for h in range(2):
-            arrived(2, 2 * k + h)
             mean = sums[6, pl.ds(2 * k + h, 1), :] * (1.0 / STIMULI)
             xc[:, h * WIDTH : (h + 1) * WIDTH] = (buf[2 * k + h].astype(F32) - mean).astype(BF16)
         layer = jnp.where(k < 4, 0, jnp.where(k < 11, 1, jnp.where(k < 18, 2, 3 + (k - 18) // 2)))
@@ -225,19 +229,14 @@
         ready = jnp.minimum((u - LAG - LATE + 1) // 2, u - (6 * PACE - 1))
         return jnp.minimum(jnp.maximum(ready, p), PAIRS)
 
-    def here_now(c):
-        part = buf.at[c, mine, :]
-        pltpu.make_async_copy(part, part, load_sem.at[c]).wait()
-        pltpu.make_async_copy(part, part, swap_recv.at[c]).wait()
-
     def send_half(c, core):
         for held, becomes, step in EDGES[0]:
             rows = [pl.ds(pl.multiple_of(b * ROWS + core * HALF, HALF), HALF) for b in (held, becomes)]
             remote(
                 buf.at[c, rows[0], :],
                 buf.at[c, rows[1], :],
-                hop_send.at[c],
-                hop_recv.at[c, kind[becomes]],
+                hop_send,
+                last_recv.at[c // 2] if kind[becomes] == 2 else hop_recv.at[kind[becomes], c],
                 at(back(STEPS[step]), p),
             ).start()
 
@@ -253,9 +252,9 @@
         pltpu.make_async_copy(part, part, swap_recv.at[c]).wait()
         send_half(c, other)
 
-    @pl.loop(EARLY, CHUNKS)
-    def _(c):
-        here_now(c)
+    rest = buf.at[pl.ds(EARLY, CHUNKS - EARLY), mine, :]
+    pltpu.make_async_copy(rest, rest, load_sem.at[EARLY]).wait()
+    pltpu.make_async_copy(rest, rest, swap_recv.at[EARLY]).wait()
 
     for c in range(CHUNKS):
         total = jnp.sum(buf[c, OWN * ROWS : (OWN + 1) * ROWS, :].astype(F32), axis=0, keepdims=True)
@@ -272,7 +271,7 @@
         def _():
             send_own(u + EARLY)
 
-        for depth in (1, 2):
+        for depth in (2, 1):
             c = u - (depth - 1) * LAG
 
             @pl.when((c >= first) & (c < CHUNKS))
@@ -318,7 +317,7 @@
                         share(i, j, to).start()
 
     def share(i, j, to):
-        return remote(pack.at[i, j % 2, to], rrx.at[j], rs_send.at[i, j % 2, to], rs_recv.at[j], at(BLOCKS[j], to))
+        return remote(pack.at[i, j % 2, to], rrx.at[j], rs_send, rs_recv, at(BLOCKS[j], to))
 
     for core in (0, 1):
 
@@ -338,16 +337,15 @@
 
     def over_plane(n):
         dx, dy = plane[n]
-        return remote(row.at[0], ar1.at[me1], ar1_send.at[n], ar1_recv.at[me1], at((dx, dy, 0), p))
+        return remote(row.at[0], ar1.at[me1], ar1_send, ar1_recv, at((dx, dy, 0), p))
 
     for n in range(15):
         over_plane(n).start()
     for core in (0, 1):
         pl.when(p == core)(lambda core=core: deliver(core))
     ar1[me1] = row[0]
-    for dx, dy in plane:
-        n = lax.rem(x + dx, 4) * 4 + lax.rem(y + dy, 4)
-        pltpu.make_async_copy(ar1.at[n], ar1.at[n], ar1_recv.at[n]).wait()
+    others1 = ar1.at[pl.ds(0, 15)]
+    pltpu.make_async_copy(others1, others1, ar1_recv).wait()
     row[1] = jnp.sum(ar1[...], axis=0)
 
     column = [(dz, dc) for dz in range(4) for dc in range(2) if dz or dc]
@@ -356,15 +354,14 @@
     def over_column(n):
         dz, dc = column[n]
         return remote(
-            row.at[1], ar2.at[me2], ar2_send.at[n], ar2_recv.at[me2], at((0, 0, dz), other if dc else p)
+            row.at[1], ar2.at[me2], ar2_send, ar2_recv, at((0, 0, dz), other if dc else p)
         )
 
     for n in range(7):
         over_column(n).start()
     ar2[me2] = row[1]
-    for dz, dc in column:
-        n = lax.rem(z + dz, 4) * 2 + (other if dc else p)
-        pltpu.make_async_copy(ar2.at[n], ar2.at[n], ar2_recv.at[n]).wait()
+    others2 = ar2.at[pl.ds(0, 7)]
+    pltpu.make_async_copy(others2, others2, ar2_recv).wait()
     total = jnp.sum(ar2[...], axis=0)
 
     def pick(index, n):
@@ -374,11 +371,12 @@
     pair = lax.broadcasted_iota(jnp.int32, (32, 1), 0)
     of_text, of_vision = pair // LB, lax.rem(pair, LB)
     scale = 1.0 / jnp.sqrt(pick(32 + jnp.minimum(of_text, LA - 1), 32) * pick(40 + of_vision, 32))
-    for j in range(len(BLOCKS)):
-        if j == OWN:
-            pl.when(p != OWN // 6)(lambda: pltpu.make_async_copy(rrx.at[OWN], rrx.at[OWN], rs_recv.at[OWN]).wait())
-        else:
-            pltpu.make_async_copy(rrx.at[j], rrx.at[j], rs_recv.at[j]).wait()
+    def tiles(core, sem):
+        part = rrx.at[pl.ds(0, len(BLOCKS) - (core == OWN // 6))]
+        pltpu.make_async_copy(part, part, sem).wait()
+
+    for core in (0, 1):
+        pl.when(p == core)(lambda core=core: tiles(core, rs_recv))
     packed = ((rrx[0] + rrx[1]) + (rrx[2] + rrx[3])) + ((rrx[4] + rrx[5]) + (rrx[6] + rrx[7]))
     packed += (rrx[8] + rrx[9]) + (rrx[10] + rrx[11])
     share_sum = jnp.concatenate([packed] + [pltpu.roll(packed, 128 - g * HALF, 1) for g in (1, 2, 3)], axis=0)
@@ -393,36 +391,21 @@
     vision_self = pltpu.roll(spread, 128 - 40, 1)
     raw[32:37, :LB] = crosses[:LA, :LB] * (1.0 / jnp.sqrt(text_self[:LA] * vision_self[:LA, :LB]))
 
-    for c in range(CHUNKS):
-        if c < 2:
-            pl.when(p == 1)(lambda c=c: swap(c).wait_send())
-        else:
-            swap(c).wait_send()
-    for n in range(6):
-        mean_copy(n).wait_send()
-
-    @pl.loop(first, CHUNKS)
-    def _(c):
-        part = buf.at[c, pl.ds(0, ALL - ROWS), :]
-        pltpu.make_async_copy(part, part, hop_send.at[c]).wait()
-
-    for layer in range(6):
-        exchanged(ex_send.at[layer])
-
     def drain(core):
-        for i in range(3):
-            q = core * 3 + i
-            for j in (2 * q, 2 * q + 1):
-                for to in (0, 1):
-                    if not (j == OWN and to == core):
-                        share(i, j, to).wait_send()
+        crossed = buf.at[pl.ds(0, CHUNKS - 2 * (1 - core)), pl.ds(0, HALF), :]
+        hopped = buf.at[pl.ds(0, CHUNKS - 2 * core), pl.ds(0, ALL - ROWS), :]
+        pltpu.make_async_copy(crossed, crossed, swap_send).wait()
+        pltpu.make_async_copy(hopped, hopped, hop_send).wait()
+        tiles(core, rs_send)
 
     for core in (0, 1):
         pl.when(p == core)(lambda core=core: drain(core))
-    for n in range(15):
-        over_plane(n).wait_send()
-    for n in range(7):
-        over_column(n).wait_send()
+    means = sums.at[pl.ds(0, 6)]
+    pltpu.make_async_copy(means, means, mean_send).wait()
+    strips = acc.at[pl.ds(0, 6), pl.ds(0, 2), pl.ds(0, 8 * ROWS)]
+    pltpu.make_async_copy(strips, strips, ex_send).wait()
+    pltpu.make_async_copy(others1, others1, ar1_send).wait()
+    pltpu.make_async_copy(others2, others2, ar2_send).wait()
 
 
 def write(raw, terms, cka):
@@ -451,21 +434,22 @@
             pltpu.VMEM((2, 1, 128), F32),
             pltpu.VMEM((16, 1, 128), F32),
             pltpu.VMEM((8, 1, 128), F32),
-            dma((CHUNKS,)),
-            dma((CHUNKS,)),
-            dma((CHUNKS,)),
+            dma((EARLY + 1,)),
+            dma,
+            dma((EARLY + 1,)),
+            dma,
             dma((6,)),
+            dma,
+            dma((2, CHUNKS)),
+            dma((PAIRS,)),
+            dma,
             dma((6,)),
-            dma((CHUNKS,)),
-            dma((CHUNKS, 3)),
-            dma((6,)),
-            dma((6,)),
-            dma((3, 2, 2)),
-            dma((12,)),
-            dma((15,)),
-            dma((16,)),
-            dma((7,)),
-            dma((8,)),
+            dma,
+            dma,
+            dma,
+            dma,
+            dma,
+            dma,
         ],
         compiler_params=pltpu.CompilerParams(collective_id=0, has_side_effects=True, vmem_limit_bytes=60 * 2**20),
     )(text_features, vision_features)

time: 103 us -> 99.7 us (0.968)
  Pallas kernels: 102 us -> 98.9 us
    pallas_call x1, Pallas kernels: 101 us -> 97.5 us  [local(): pl.pallas_call(kernel, out_shape=jax.ShapeDtypeStruct((40, 128), F32), in...]
where the time goes in v4:
time: 99.7 us; the launch traced here: 99.5 us
  Pallas kernels  98.9 us (99%)
    pallas_call x1, Pallas kernels, local(): pl.pallas_call(kernel, out_shape=jax.ShapeDtypeStruct((40, 128), F32), in...  97.5 us

profile of v4, /device:TPU:1, one launch (start us, length us, event | category | flops | bytes accessed | tf_op | source)
XLA Modules:
  0.0 99.5 jit_solution(14336709574675732369)
XLA Ops:
  0.6 97.5 %shard_map.41.raw = f32[40,128]{1,0:T(8,128)} custom-call(bf16[5,32,3584]{2,1,0:T(8,128)(2,1)} %text.1, bf16[6,32,1024]{2,1,0:T(8,128)(2,1)} %vision.1), custom_call_target="tpu_custom_call" | custom-call | tf_op jit(solution)/shard_map/pallas_call | solution.py:418
  98.1 1.4 %shard_map.42 = (f32[32,30]{1,0:T(8,128)}, f32[5,6]{1,0:T(8,128)}) custom-call(f32[40,128]{1,0:T(8,128)} %shard_map.41.raw), custom_call_target="tpu_custom_call" | custom-call | tf_op jit(solution)/shard_map/pallas_call | solution.py:456

commit v5 on v4

--- a/solution.py
+++ b/solution.py
@@ -24,7 +24,7 @@
 PAIRS = CHUNKS // 2
 ROWS, HALF = 64, 32
 ALL = len(BLOCKS) * ROWS
-EARLY, LAG, LATE, PACE = 4, 4, 3, 4
+EARLY, LAG, LATE, PACE = 4, 4, 4, 4
 LAST = (3, 10, 17, 19, 21, 23)
 F32, BF16 = jnp.float32, jnp.bfloat16
 MESH = pl.DeviceIdType.MESH

time: 99.7 us -> 99.4 us (level)
  no operation moved by 1% of the time
where the time goes in v5:
time: 99.4 us; the launch traced here: 99.2 us
  Pallas kernels  98.6 us (99%)
    pallas_call x1, Pallas kernels, local(): pl.pallas_call(kernel, out_shape=jax.ShapeDtypeStruct((40, 128), F32), in...  97.2 us

profile of v5, /device:TPU:1, one launch (start us, length us, event | category | flops | bytes accessed | tf_op | source)
XLA Modules:
  0.0 99.2 jit_solution(8955277145482834620)
XLA Ops:
  0.6 97.2 %shard_map.41.raw = f32[40,128]{1,0:T(8,128)} custom-call(bf16[5,32,3584]{2,1,0:T(8,128)(2,1)} %text.1, bf16[6,32,1024]{2,1,0:T(8,128)(2,1)} %vision.1), custom_call_target="tpu_custom_call" | custom-call | tf_op jit(solution)/shard_map/pallas_call | solution.py:418
  97.8 1.4 %shard_map.42 = (f32[32,30]{1,0:T(8,128)}, f32[5,6]{1,0:T(8,128)}) custom-call(f32[40,128]{1,0:T(8,128)} %shard_map.41.raw), custom_call_target="tpu_custom_call" | custom-call | tf_op jit(solution)/shard_map/pallas_call | solution.py:456
